TPU v7x, 32 devices: a whole 2x2x4 slice. The times are simulated.
32 devices in a mesh: tok: 8 (over z, y), voc: 4 (over x, core).
Axes of the slice: x: 2, y: 2, z: 4, core: 2. Of those that a mesh axis runs over, the one named last changes fastest.
Arguments:
- hidden: bfloat16 [96, 4096], P(('tok', 'voc'))
- head_weight: bfloat16 [4096, 16032], P(None, ('tok', 'voc'))
- actions: int32 [96], P(('tok', 'voc')), may hold values from 0 to 16031
- old_logp: bfloat16 [96], P(('tok', 'voc')), may hold values from -80 to 1
- advantage: bfloat16 [96], P(('tok', 'voc')), may hold values from -4 to 4
- loss_mask: int32 [96], P(('tok', 'voc')), may hold values 0 or 1
Outputs:
- grad_weight: bfloat16 [4096, 16032], P(None, ('tok', 'voc'))
- grad_hidden: float32 [96, 4096], P(('tok', 'voc'))
All inputs are finite; a program needn't handle non-finite values. No bound on the sum of `loss_mask` on one device may be relied on, other than what follows from the above.
Results may differ from a plain program's by a relative error of at most 0.0047.
Values may be sent and summed in bfloat16 or wider, within the bound.
A program may use at most 128 MiB of HBM per device.

v0:
```python
import jax
import jax.numpy as jnp
from jax import lax
from jax.sharding import PartitionSpec as P


def per_device(hidden, head_weight, actions, old_logp, advantage, loss_mask):
    hidden_all, old_all, advant_all = (
        lax.all_gather(hidden, ("tok", "voc"), axis=0, tiled=True),
        lax.all_gather(old_logp, ("tok", "voc"), axis=0, tiled=True),
        lax.all_gather(advantage, ("tok", "voc"), axis=0, tiled=True),
    )
    action_all, mask_all = (
        lax.all_gather(actions, ("tok", "voc"), axis=0, tiled=True),
        lax.all_gather(loss_mask, ("tok", "voc"), axis=0, tiled=True),
    )
    width = head_weight.shape[1]
    logits = jnp.dot(hidden_all, head_weight, preferred_element_type=jnp.float32)
    first_col = lax.axis_index(("tok", "voc")) * width
    columns = first_col + lax.broadcasted_iota(jnp.int32, logits.shape, 1)
    matches = columns == action_all[:, None]
    target_part = jnp.sum(jnp.where(matches, logits, 0.0), axis=1)
    top = lax.pmax(jnp.max(logits, axis=1), ("tok", "voc"))
    shifted = jnp.exp(logits - top[:, None])
    sumexp, moment, target = lax.psum(
        (jnp.sum(shifted, axis=1), jnp.sum(shifted * logits, axis=1), target_part), ("tok", "voc")
    )
    lse = top + jnp.log(sumexp)
    mean_logit = moment / sumexp
    advant = advant_all.astype(jnp.float32)
    ratio = jnp.exp(target - lse - old_all.astype(jnp.float32))
    clipped = (advant > 0.0) & (ratio > 1.2) | (advant < 0.0) & (ratio < 0.8)
    active = jnp.where(clipped, 0.0, 1.0).astype(jnp.float32)
    weights = mask_all.astype(jnp.float32)
    policy = -advant * ratio * active * weights
    probability = jnp.exp(logits - lse[:, None])
    onehot = matches.astype(jnp.float32)
    dlogits = policy[:, None] * (onehot - probability) + 0.05 * weights[:, None] * probability * (
        logits - mean_logit[:, None]
    )
    dlogits = dlogits.astype(jnp.bfloat16)
    partial_rows = lax.psum_scatter(
        lax.dot_general(
            dlogits, head_weight, (((1,), (1,)), ((), ())), preferred_element_type=jnp.float32
        ),
        "tok",
        scatter_dimension=0,
        tiled=True,
    )
    grad_hidden = lax.psum_scatter(partial_rows, "voc", scatter_dimension=0, tiled=True)
    grad_weight = lax.dot_general(
        hidden_all, dlogits, (((0,), (0,)), ((), ())), preferred_element_type=jnp.float32
    ).astype(jnp.bfloat16)
    return (grad_weight, grad_hidden)


def solution(mesh):
    placed = (
        P(("tok", "voc"), None),
        P(None, ("tok", "voc")),
        P(("tok", "voc")),
        P(("tok", "voc")),
        P(("tok", "voc")),
        P(("tok", "voc")),
    )
    return jax.shard_map(
        per_device,
        mesh=mesh,
        in_specs=placed,
        out_specs=(P(None, ("tok", "voc")), P(("tok", "voc"), None)),
        check_vma=False,
    )
```

profile of v0, /device:TPU:0, one launch (start us, length us, event | category | flops | bytes accessed | tf_op | source)
XLA Modules:
  0.0 323.1 jit_solution(7266715647205631639)
XLA Ops:
  7.2 0.0 copy-start.1
  7.2 0.0 all-reduce.12.cloned.1.call-start
  7.3 46.5 %all-gather = bf16[32,3,4096]{2,1,0:T(4,128)(2,1)S(1)} all-gather(bf16[1,3,4096]{2,1,0:T(4,128)(2,1)} %bitcast.11), channel_id=1, replica_groups=mesh['tok'=8,'voc'=4] {'tok','voc'}, dimensions={0}, use_global_device_ids=true | all-gather | bytes 811008 | tf_op jit(solution)/shard_map/all_gather | solution.py:9
  53.7 0.7 reshape.20
  54.4 3.6 %fusion.12 = (f32[96]{0:T(128)S(1)}, f32[96,501]{1,0:T(8,128)S(1)}) fusion(bf16[96,4096]{1,0:T(8,128)(2,1)S(1)} %reshape.20, bf16[4096,501]{0,1:T(8,128)(2,1)} %param.7), kind=kOutput, calls=%fused_computation.21 | convolution fusion | flops 394050432 | bytes 5083392 | tf_op jit(solution)/shard_map/dot_general | solution.py:18
  58.0 36.9 %pmax.7 = f32[96]{0:T(128)S(1)} all-reduce(f32[96]{0:T(128)S(1)} %get-tuple-element.16), channel_id=1, replica_groups=mesh['tok'=8,'voc'=4] {'tok','voc'}, use_global_device_ids=true, to_apply=%region_3.4 | all-reduce | flops 96 | bytes 768 | tf_op jit(solution)/shard_map/pmax | solution.py:23
  94.9 0.0 copy-done.1
  94.9 0.2 dynamic-update-slice.2
  95.1 0.0 copy-done.2
  95.1 0.2 dynamic-update-slice
  95.4 41.1 %all-reduce.9 = (bf16[96]{0:T(256)(128)(2,1)S(1)}, bf16[96]{0:T(256)(128)(2,1)S(1)}) all-reduce(bf16[96]{0:T(256)(128)(2,1)S(1)} %dynamic-update-slice.2, bf16[96]{0:T(256)(128)(2,1)S(1)} %dynamic-update-slice), channel_id=1, replica_groups=mesh['tok'=8,'voc'=4] {'tok','voc'}, use_global_device_ids=true, to_apply=%add.2 | all-reduce | flops 192 | bytes 768
  136.5 0.2 dynamic-update-slice.1
  136.7 0.2 dynamic-update-slice.3
  137.0 39.5 %all-reduce.7 = (s32[96]{0:T(128)S(1)}, s32[96]{0:T(128)S(1)}) all-reduce(s32[96]{0:T(128)S(1)} %dynamic-update-slice.1, s32[96]{0:T(128)S(1)} %dynamic-update-slice.3), channel_id=1, replica_groups=mesh['tok'=8,'voc'=4] {'tok','voc'}, use_global_device_ids=true, to_apply=%add.1 | all-reduce | flops 192 | bytes 1536
  176.4 0.2 fusion.7
  176.7 40.5 %all-reduce.8 = (f32[96]{0:T(128)S(1)}, f32[96]{0:T(128)S(1)}, f32[96]{0:T(128)S(1)}) all-reduce(f32[96]{0:T(128)S(1)} %get-tuple-element.3, f32[96]{0:T(128)S(1)} %get-tuple-element.2, f32[96]{0:T(128)S(1)} %get-tuple-element.4), channel_id=1, replica_groups=mesh['tok'=8,'voc'=4] {'tok','voc'}, use_global_device_ids=true, to_apply=%region_7.8 | all-reduce | flops 288 | bytes 2304 | tf_op jit(solution)/shard_map/psum | solution.py:25
  217.1 0.0 copy-start
  217.2 3.2 fusion.9
  220.3 46.1 %fusion = f32[16,4096]{1,0:T(8,128)S(1)} fusion(f32[96,4096]{1,0:T(8,128)S(1)} %fusion.9), kind=kCustom, calls=%all-reduce-scatter | all-reduce-scatter fusion | flops 524289 | bytes 1835520
  266.5 4.3 %collective-permute-start = (f32[16,4096]{1,0:T(8,128)S(1)}, f32[16,4096]{1,0:T(8,128)S(1)}, u32[]{:S(2)}, u32[]{:S(2)}) collective-permute-start(f32[16,4096]{1,0:T(8,128)S(1)} %fusion), channel_id=1, source_target_pairs={{0,4},{4,8},{8,12},{12,16},{16,20},{20,24},{24,28},{1,5},{5,9},{9,... | collective-permute-start | bytes 786440
  270.8 2.7 collective-permute-start.1
  273.5 0.6 dynamic-slice.6
  274.7 2.6 collective-permute-done.1
  277.3 0.0 collective-permute-done
  277.3 0.6 concatenate
  278.0 0.0 copy-start.5
  278.0 0.7 constant_dynamic-slice_fusion
  278.7 0.0 all-reduce.12.cloned.1.call-update
  278.7 3.4 %fusion.1 = bf16[4096,501]{0,1:T(8,128)(2,1)} fusion(bf16[96,4096]{1,0:T(8,128)(2,1)S(1)} %reshape.20, f32[96,501]{1,0:T(8,128)S(1)} %get-tuple-element.17, f32[96]{0:T(128)S(1)} %get-tuple-element.14, f32[96]{0:T(128)S(1)} %get-tuple-element.15, f32[96]{0:T(128)S(1)} %get-tuple-element.13, f32[96]{0:T(128)S(1)} %get-tuple-element.12, ...), kind=kOutput, calls=%fused_computation.1 | convolution fusion | flops 396535488 | bytes 5086932 | tf_op jit(solution)/shard_map/dot_general | solution.py:51
  282.1 0.6 dynamic-slice.2
  283.4 31.4 %all-reduce.12.cloned.1.call-done = f32[12,4096]{1,0:T(8,128)} async-done(((f32[12,4096]{1,0:T(8,128)}), f32[12,4096]{1,0:T(8,128)}) %all-reduce.12.cloned.1.call-update) | async-done | bytes 196624
  314.7 1.6 constant_dynamic-slice_fusion.1
  (14 shorter events, 0.1 us)
Async XLA Ops:
  7.2 87.7 %copy-start.1 = (bf16[3]{0:T(256)(128)(2,1)S(1)}, bf16[3]{0:T(256)(128)(2,1)}, u32[]{:S(2)}) copy-start(bf16[3]{0:T(256)(128)(2,1)} %param.9) | copy-start | bytes 22
  7.2 88.0 %copy-start.2 = (bf16[3]{0:T(256)(128)(2,1)S(1)}, bf16[3]{0:T(256)(128)(2,1)}, u32[]{:S(2)}) copy-start(bf16[3]{0:T(256)(128)(2,1)} %param.10) | copy-start | bytes 22
  7.2 129.3 %copy-start.3 = (s32[3]{0:T(128)S(1)}, s32[3]{0:T(128)}, u32[]{:S(2)}) copy-start(s32[3]{0:T(128)} %param.8) | copy-start | bytes 40
  7.2 129.5 %copy-start.4 = (s32[3]{0:T(128)S(1)}, s32[3]{0:T(128)}, u32[]{:S(2)}) copy-start(s32[3]{0:T(128)} %param.11) | copy-start | bytes 40
  7.2 307.5 %all-reduce.12.cloned.1.call-start = ((), (), s32[]{:S(2)}) async-start(), calls=%async_computation | async-start | bytes 524288
  217.1 56.3 %copy-start = (u32[32]{0:T(128)S(1)}, u32[32]{0:T(128)}, u32[]{:S(2)}) copy-start(u32[32]{0:T(128)} %constant.50) | copy-start | bytes 388
  266.5 10.9 %collective-permute-start = (f32[16,4096]{1,0:T(8,128)S(1)}, f32[16,4096]{1,0:T(8,128)S(1)}, u32[]{:S(2)}, u32[]{:S(2)}) collective-permute-start(f32[16,4096]{1,0:T(8,128)S(1)} %fusion), channel_id=1, source_target_pairs={{0,4},{4,8},{8,12},{12,16},{16,20},{20,24},{24,28},{1,5},{5,9},{9,... | collective-permute-start | bytes 786440
  270.8 6.6 %collective-permute-start.1 = (f32[12,4096]{1,0:T(8,128)S(1)}, f32[12,4096]{1,0:T(8,128)S(1)}, u32[]{:S(2)}, u32[]{:S(2)}) collective-permute-start(f32[12,4096]{1,0:T(8,128)S(1)} %slice), channel_id=1, source_target_pairs={{0,8},{4,12},{8,16},{12,20},{16,24},{20,28},{1,9},{5,13},{9,17},{1... | collective-permute-start | bytes 589832
  278.0 4.1 %copy-start.5 = (u32[32]{0:T(128)S(1)}, u32[32]{0:T(128)}, u32[]{:S(2)}) copy-start(u32[32]{0:T(128)} %constant.54) | copy-start | bytes 388
Sparse Core Ops, SparseCore 0:
  278.9 35.7 all-reduce.11
where the time goes:
time: 324 us; the launch traced here: 323 us
  blocking collectives  250 us (77%)
  waiting for transfers between devices  34 us (10%)
  between operations  15.5 us (5%)
  matrix products  10.2 us (3%)
  starting transfers between devices  7 us (2%)
  local copies, waits for them, and re-layouts  5.77 us (2%)
    unnamed x3, blocking collectives  127 us
    all_gather x1, blocking collectives, per_device(): lax.all_gather(hidden, ('tok', 'voc'), axis=0, tiled=True)  46.5 us
    psum x1, blocking collectives, per_device(): lax.psum((jnp.sum(shifted, axis=1), jnp.sum(shifted * logits, axis=1), ta...  40.5 us
    pmax x1, blocking collectives, per_device(): top = lax.pmax(jnp.max(logits, axis=1), ('tok', 'voc'))  36.9 us
    unnamed x4, waiting for transfers between devices  34 us
    unnamed x3, starting transfers between devices  7 us
  transfers between devices with their start and end apart: 3, of which 2 were waited for; matrix products, arithmetic and copies ran while one was open for 1% of the time, Pallas kernels for 0%

commit v1 on v0

--- a/solution.py
+++ b/solution.py
@@ -22,8 +22,11 @@
     target_part = jnp.sum(jnp.where(matches, logits, 0.0), axis=1)
     top = lax.pmax(jnp.max(logits, axis=1), ("tok", "voc"))
     shifted = jnp.exp(logits - top[:, None])
-    sumexp, moment, target = lax.psum(
-        (jnp.sum(shifted, axis=1), jnp.sum(shifted * logits, axis=1), target_part), ("tok", "voc")
+    sumexp, moment, target = jax.lax.psum(
+        jax.lax.psum(
+            (jnp.sum(shifted, axis=1), jnp.sum(shifted * logits, axis=1), target_part), "tok"
+        ),
+        "voc",
     )
     lse = top + jnp.log(sumexp)
     mean_logit = moment / sumexp

time: 324 us -> 308 us (0.951)
  blocking collectives: 250 us -> 234 us
    psum x1 -> x2, blocking collectives: 40.5 us -> 26.2 us  [the longest x1 20.4 us: per_device(): jax.lax.psum((jnp.sum(shifted, axis=1), jnp.sum(shifted * logits, axis=1)...]
where the time goes in v1:
time: 308 us; the launch traced here: 307 us
  blocking collectives  234 us (76%)
  waiting for transfers between devices  36.5 us (12%)
  between operations  15.5 us (5%)
  matrix products  10.2 us (3%)
  local copies, waits for them, and re-layouts  5.76 us (2%)
  starting transfers between devices  4.78 us (2%)
    unnamed x3, blocking collectives  125 us
    all_gather x1, blocking collectives, per_device(): lax.all_gather(hidden, ('tok', 'voc'), axis=0, tiled=True)  46.5 us
    pmax x1, blocking collectives, per_device(): top = lax.pmax(jnp.max(logits, axis=1), ('tok', 'voc'))  36.8 us
    unnamed x4, waiting for transfers between devices  36.5 us
    psum x1, blocking collectives, per_device(): jax.lax.psum((jnp.sum(shifted, axis=1), jnp.sum(shifted * logits, axis=1)...  20.4 us
  transfers between devices with their start and end apart: 3, of which 2 were waited for; matrix products, arithmetic and copies ran while one was open for 1% of the time, Pallas kernels for 0%

profile of v1, /device:TPU:0, one launch (start us, length us, event | category | flops | bytes accessed | tf_op | source)
XLA Modules:
  0.0 307.4 jit_solution(1751652609228850190)
XLA Ops:
  7.2 0.0 copy-start.1
  7.2 0.0 copy-start.2
  7.2 0.0 all-reduce.13.cloned.1.call-start
  7.3 46.5 %all-gather = bf16[32,3,4096]{2,1,0:T(4,128)(2,1)S(1)} all-gather(bf16[1,3,4096]{2,1,0:T(4,128)(2,1)} %bitcast.11), channel_id=1, replica_groups=mesh['tok'=8,'voc'=4] {'tok','voc'}, dimensions={0}, use_global_device_ids=true | all-gather | bytes 811008 | tf_op jit(solution)/shard_map/all_gather | solution.py:9
  53.7 0.7 reshape.20
  54.4 3.6 %fusion.12 = (f32[96]{0:T(128)S(1)}, f32[96,501]{1,0:T(8,128)S(1)}) fusion(bf16[96,4096]{1,0:T(8,128)(2,1)S(1)} %reshape.20, bf16[4096,501]{0,1:T(8,128)(2,1)} %param.7), kind=kOutput, calls=%fused_computation.21 | convolution fusion | flops 394050432 | bytes 5083392 | tf_op jit(solution)/shard_map/dot_general | solution.py:18
  58.0 36.8 %pmax.7 = f32[96]{0:T(128)S(1)} all-reduce(f32[96]{0:T(128)S(1)} %get-tuple-element.19), channel_id=1, replica_groups=mesh['tok'=8,'voc'=4] {'tok','voc'}, use_global_device_ids=true, to_apply=%region_4.5 | all-reduce | flops 96 | bytes 768 | tf_op jit(solution)/shard_map/pmax | solution.py:23
  94.9 0.2 dynamic-update-slice.2
  95.1 0.2 dynamic-update-slice
  95.3 41.1 %all-reduce.10 = (bf16[96]{0:T(256)(128)(2,1)S(1)}, bf16[96]{0:T(256)(128)(2,1)S(1)}) all-reduce(bf16[96]{0:T(256)(128)(2,1)S(1)} %dynamic-update-slice.2, bf16[96]{0:T(256)(128)(2,1)S(1)} %dynamic-update-slice), channel_id=1, replica_groups=mesh['tok'=8,'voc'=4] {'tok','voc'}, use_global_device_ids=true, to_apply=%add.2 | all-reduce | flops 192 | bytes 768
  136.5 0.2 dynamic-update-slice.1
  136.7 0.2 dynamic-update-slice.3
  136.9 39.5 %all-reduce.7 = (s32[96]{0:T(128)S(1)}, s32[96]{0:T(128)S(1)}) all-reduce(s32[96]{0:T(128)S(1)} %dynamic-update-slice.1, s32[96]{0:T(128)S(1)} %dynamic-update-slice.3), channel_id=1, replica_groups=mesh['tok'=8,'voc'=4] {'tok','voc'}, use_global_device_ids=true, to_apply=%add.1 | all-reduce | flops 192 | bytes 1536
  176.4 0.2 fusion.7
  176.6 20.4 %all-reduce.8 = (f32[96]{0:T(128)S(1)}, f32[96]{0:T(128)S(1)}, f32[96]{0:T(128)S(1)}) all-reduce(f32[96]{0:T(128)S(1)} %get-tuple-element.3, f32[96]{0:T(128)S(1)} %get-tuple-element.2, f32[96]{0:T(128)S(1)} %get-tuple-element.4), channel_id=1, replica_groups=mesh['tok'=8,'voc'=4] {'tok'}, use_global_device_ids=true, to_apply=%region_9.10 | all-reduce | flops 288 | bytes 2304 | tf_op jit(solution)/shard_map/psum | solution.py:26
  197.0 5.8 %all-reduce.9 = (f32[96]{0:T(128)S(1)}, f32[96]{0:T(128)S(1)}, f32[96]{0:T(128)S(1)}) all-reduce(f32[96]{0:T(128)S(1)} %get-tuple-element.7, f32[96]{0:T(128)S(1)} %get-tuple-element.8, f32[96]{0:T(128)S(1)} %get-tuple-element.9), channel_id=1, replica_groups=mesh['tok'=8,'voc'=4] {'voc'}, use_global_device_ids=true, to_apply=%region_10.11 | all-reduce | flops 288 | bytes 2304 | tf_op jit(solution)/shard_map/psum | solution.py:25
  202.8 0.0 copy-start
  202.9 3.2 %fusion.9 = f32[96,4096]{1,0:T(8,128)S(1)} fusion(bf16[4096,501]{0,1:T(8,128)(2,1)} %param.7, f32[96,501]{1,0:T(8,128)S(1)} %get-tuple-element.20, f32[96]{0:T(128)S(1)} %get-tuple-element.17, f32[96]{0:T(128)S(1)} %get-tuple-element.18, f32[96]{0:T(128)S(1)} %get-tuple-element.16, f32[96]{0:T(128)S(1)} %get-tuple-element.15, s32[501]{0:T(512)S(1)} %iota_add_fusion, ...), kind=kOutput, calls=%fused_computation.20 | convolution fusion | flops 394483392 | bytes 5873364 | tf_op jit(solution)/shard_map/dot_general | solution.py:46
  206.0 44.3 %fusion = f32[16,4096]{1,0:T(8,128)S(1)} fusion(f32[96,4096]{1,0:T(8,128)S(1)} %fusion.9), kind=kCustom, calls=%all-reduce-scatter | all-reduce-scatter fusion | flops 524289 | bytes 1835520
  250.3 3.4 %collective-permute-start = (f32[16,4096]{1,0:T(8,128)S(1)}, f32[16,4096]{1,0:T(8,128)S(1)}, u32[]{:S(2)}, u32[]{:S(2)}) collective-permute-start(f32[16,4096]{1,0:T(8,128)S(1)} %fusion), channel_id=1, source_target_pairs={{0,4},{4,8},{8,12},{12,16},{16,20},{20,24},{24,28},{1,5},{5,9},{9,... | collective-permute-start | bytes 786440
  253.8 1.3 collective-permute-start.1
  255.1 0.6 dynamic-slice.6
  256.4 2.9 collective-permute-done.1
  259.3 0.0 collective-permute-done
  259.3 0.6 concatenate
  259.9 0.0 copy-start.5
  259.9 0.7 constant_dynamic-slice_fusion
  260.6 0.0 all-reduce.13.cloned.1.call-update
  260.7 3.4 %fusion.1 = bf16[4096,501]{0,1:T(8,128)(2,1)} fusion(bf16[96,4096]{1,0:T(8,128)(2,1)S(1)} %reshape.20, f32[96,501]{1,0:T(8,128)S(1)} %get-tuple-element.20, f32[96]{0:T(128)S(1)} %get-tuple-element.17, f32[96]{0:T(128)S(1)} %get-tuple-element.18, f32[96]{0:T(128)S(1)} %get-tuple-element.16, f32[96]{0:T(128)S(1)} %get-tuple-element.15, ...), kind=kOutput, calls=%fused_computation.1 | convolution fusion | flops 396535488 | bytes 5086932 | tf_op jit(solution)/shard_map/dot_general | solution.py:54
  264.0 0.6 dynamic-slice.2
  265.3 33.6 %all-reduce.13.cloned.1.call-done = f32[12,4096]{1,0:T(8,128)} async-done(((f32[12,4096]{1,0:T(8,128)}), f32[12,4096]{1,0:T(8,128)}) %all-reduce.13.cloned.1.call-update) | async-done | bytes 196624
  298.9 1.6 constant_dynamic-slice_fusion.1
  (15 shorter events, 0.1 us)
Async XLA Ops:
  7.2 87.7 %copy-start.1 = (bf16[3]{0:T(256)(128)(2,1)S(1)}, bf16[3]{0:T(256)(128)(2,1)}, u32[]{:S(2)}) copy-start(bf16[3]{0:T(256)(128)(2,1)} %param.9) | copy-start | bytes 22
  7.2 87.9 %copy-start.2 = (bf16[3]{0:T(256)(128)(2,1)S(1)}, bf16[3]{0:T(256)(128)(2,1)}, u32[]{:S(2)}) copy-start(bf16[3]{0:T(256)(128)(2,1)} %param.10) | copy-start | bytes 22
  7.2 129.3 %copy-start.3 = (s32[3]{0:T(128)S(1)}, s32[3]{0:T(128)}, u32[]{:S(2)}) copy-start(s32[3]{0:T(128)} %param.8) | copy-start | bytes 40
  7.2 129.5 %copy-start.4 = (s32[3]{0:T(128)S(1)}, s32[3]{0:T(128)}, u32[]{:S(2)}) copy-start(s32[3]{0:T(128)} %param.11) | copy-start | bytes 40
  7.2 291.7 %all-reduce.13.cloned.1.call-start = ((), (), s32[]{:S(2)}) async-start(), calls=%async_computation | async-start | bytes 524288
  202.8 52.3 %copy-start = (u32[32]{0:T(128)S(1)}, u32[32]{0:T(128)}, u32[]{:S(2)}) copy-start(u32[32]{0:T(128)} %constant.50) | copy-start | bytes 388
  250.3 8.9 %collective-permute-start = (f32[16,4096]{1,0:T(8,128)S(1)}, f32[16,4096]{1,0:T(8,128)S(1)}, u32[]{:S(2)}, u32[]{:S(2)}) collective-permute-start(f32[16,4096]{1,0:T(8,128)S(1)} %fusion), channel_id=1, source_target_pairs={{0,4},{4,8},{8,12},{12,16},{16,20},{20,24},{24,28},{1,5},{5,9},{9,... | collective-permute-start | bytes 786440
  253.8 5.5 %collective-permute-start.1 = (f32[12,4096]{1,0:T(8,128)S(1)}, f32[12,4096]{1,0:T(8,128)S(1)}, u32[]{:S(2)}, u32[]{:S(2)}) collective-permute-start(f32[12,4096]{1,0:T(8,128)S(1)} %slice), channel_id=1, source_target_pairs={{0,8},{4,12},{8,16},{12,20},{16,24},{20,28},{1,9},{5,13},{9,17},{1... | collective-permute-start | bytes 589832
  259.9 4.1 %copy-start.5 = (u32[32]{0:T(128)S(1)}, u32[32]{0:T(128)}, u32[]{:S(2)}) copy-start(u32[32]{0:T(128)} %constant.54) | copy-start | bytes 388
Sparse Core Ops, SparseCore 0:
  260.8 38.0 all-reduce.12
